TPU v7x, 32 devices: a whole 2x2x4 slice. The times are simulated.
32 devices in a mesh: row: 4 (over y, core), col: 8 (over z, x).
Axes of the slice: x: 2, y: 2, z: 4, core: 2. Of those that a mesh axis runs over, the one named last changes fastest.
Arguments:
- values: bfloat16 [8192, 128], P('row'), may hold values from -30 to 30
- points0: bfloat16 [2, 8192], P(None, 'row'), may hold values from 0 to 1
- points1: bfloat16 [2, 2048], P(None, 'row'), may hold values from 0 to 1
- points2: bfloat16 [2, 256], P(None, 'row'), may hold values from 0 to 1
- tiles_a0: int32 [4, 8, 2, 48], P('row', 'col'), may hold values from 0 to 15, as said below
- tiles_e1: int32 [4, 8, 2, 20], P('row', 'col'), may hold values from 0 to 15, as said below
- tiles_a1: int32 [4, 8, 2, 4], P('row', 'col'), may hold values from 0 to 3, as said below
- factor: bfloat16 [256, 256], P('row', 'col'), as said below
Outputs:
- fine_coef: float32 [8192, 128], P(('row', 'col'))
- mid_coef: float32 [2048, 128], P('col')
- coarse_coef: float32 [256, 128], P('row')
- norms: float32 [1], replicated
Inputs may be any that keep to these rules, and one draw needn't show every extreme that they name: `tiles_a0`: within each block the 48 listed tile pairs are distinct; tile rows are below 16 and tile columns below 8. `tiles_e1`: within each block the 20 listed tile pairs are distinct; tile rows are below 16 and tile columns below 2. `tiles_a1`: within each block the 4 listed tile pairs are distinct; tile rows are below 4 and tile columns below 2. `factor`: upper triangular; diagonal entries from 1 to 2.
All inputs are finite; a program needn't handle non-finite values.
Results may differ from a plain program's by a relative error of at most 0.0042.
Values may be sent and summed in bfloat16 or wider, within the bound.
A program may use at most 64 MiB of HBM per device.

v0:
```python
import math
import jax
import jax.numpy as jnp
from jax import lax
from jax.sharding import PartitionSpec as P

TILE = 128
support_fine = 0.35
support_mid = 0.55
support_coarse = 0.8


def spread(x, axis, root):
    mine = lax.axis_index(axis) == root
    return lax.psum(jnp.where(mine, x, jnp.zeros_like(x)), axis)


def wendland(left_pts, right_pts, support):
    left = left_pts.astype(jnp.float32)
    right = right_pts.astype(jnp.float32)
    across = left[0][..., :, None] - right[0][..., None, :]
    upward = left[1][..., :, None] - right[1][..., None, :]
    ratio_t = jnp.sqrt(across * across + upward * upward) / support
    margin = jnp.maximum(1.0 - ratio_t, 0.0)
    squared = margin * margin
    return (squared * squared * (4.0 * ratio_t + 1.0)).astype(jnp.bfloat16)


def listed_terms(row_pts, col_pts, listing, vector, support, flipped):
    row_tiles = row_pts.reshape(2, -1, TILE)
    col_tiles = col_pts.reshape(2, -1, TILE)
    listed = listing.shape[-1]
    group = math.gcd(listed, 32)
    order = listing.reshape(2, listed // group, group)
    fields = vector.shape[-1]
    inputs = vector.reshape(-1, TILE, fields)
    target = col_tiles.shape[1] if flipped else row_tiles.shape[1]
    total = jnp.zeros((target, TILE, fields), jnp.float32)

    def add_group(total, pair):
        tile_rows, tile_cols = pair
        kernel = wendland(row_tiles[:, tile_rows], col_tiles[:, tile_cols], support)
        if flipped:
            contrib = jnp.einsum(
                "gij,gir->gjr", kernel, inputs[tile_rows], preferred_element_type=jnp.float32
            )
            return (total.at[tile_cols].add(contrib), None)
        contrib = jnp.einsum(
            "gij,gjr->gir", kernel, inputs[tile_cols], preferred_element_type=jnp.float32
        )
        return (total.at[tile_rows].add(contrib), None)

    total, unused = lax.scan(add_group, total, (order[0], order[1]))
    return total.reshape(-1, fields)


def per_device(values, points0, points1, points2, tiles_a0, tiles_e1, tiles_a1, factor):
    row_count = lax.axis_size("row")
    col_count = lax.axis_size("col")
    col_id = lax.axis_index("col")
    col_per_row = col_count // row_count
    rows_fine, fields = values.shape
    rows_mid = points1.shape[1]
    share = rows_fine // col_count
    cols_fine = rows_fine // col_per_row
    cols_mid = rows_mid // col_per_row
    source = col_id // col_per_row
    part_index = col_id % col_per_row
    value_piece = lax.dynamic_slice_in_dim(values, part_index * cols_fine, cols_fine, 0)
    fine_piece = lax.dynamic_slice_in_dim(points0, part_index * cols_fine, cols_fine, 1)
    mid_piece = lax.dynamic_slice_in_dim(points1, part_index * cols_mid, cols_mid, 1)
    value_cols, fine_cols, mid_cols = (
        spread(value_piece, "row", source),
        spread(fine_piece, "row", source),
        spread(mid_piece, "row", source),
    )
    scale_a0 = (rows_fine / (col_count * tiles_a0.shape[-1] * TILE * TILE)) ** 0.5
    scale_e1 = (rows_fine / (col_count * tiles_e1.shape[-1] * TILE * TILE)) ** 0.5
    scale_a1 = (rows_mid / (col_count * tiles_a1.shape[-1] * TILE * TILE)) ** 0.5
    scale_e2 = (1.0 / (rows_mid * row_count)) ** 0.5
    fine_data = values.astype(jnp.float32)
    own_data = lax.dynamic_slice_in_dim(values, col_id * share, share, 0).astype(jnp.float32)
    product_part = listed_terms(points0, fine_cols, tiles_a0[0, 0], value_cols, support_fine, False)
    product_whole = lax.psum(product_part, "col")
    fine_residual = fine_data - 0.5 * (scale_a0 * product_whole)
    fine_square = jnp.sum(fine_residual * fine_residual)
    restrict_part = listed_terms(
        points0, mid_cols, tiles_e1[0, 0], fine_residual.astype(jnp.bfloat16), support_mid, True
    )
    restrict_sum = lax.psum(restrict_part, "row")
    mid_data = scale_e1 * restrict_sum
    mid_part = listed_terms(
        points1, mid_cols, tiles_a1[0, 0], mid_data.astype(jnp.bfloat16), support_mid, False
    )
    mid_whole = (scale_a1 * lax.psum(mid_part, "col")).astype(jnp.bfloat16)
    mid_slice = lax.dynamic_slice_in_dim(mid_whole, part_index * cols_mid, cols_mid, 0)
    mid_turned = spread(mid_slice, "row", source)
    mid_residual = mid_data - 0.5 * mid_turned.astype(jnp.float32)
    coarse_kernel = wendland(points2, mid_cols, support_coarse)
    coarse_part = jnp.dot(
        coarse_kernel, mid_residual.astype(jnp.bfloat16), preferred_element_type=jnp.float32
    )
    coarse_sum = lax.psum(coarse_part, "col")
    coarse_data = (scale_e2 * coarse_sum).astype(jnp.bfloat16)
    halfway_part = lax.dot_general(
        factor, coarse_data, (((0,), (0,)), ((), ())), preferred_element_type=jnp.float32
    )
    halfway = lax.psum(halfway_part, "row").astype(jnp.bfloat16)
    coarse_part_two = jnp.dot(factor, halfway, preferred_element_type=jnp.float32)
    coarse_coef = lax.psum(coarse_part_two, "col")
    prolong_part = lax.dot_general(
        coarse_kernel,
        coarse_coef.astype(jnp.bfloat16),
        (((0,), (0,)), ((), ())),
        preferred_element_type=jnp.float32,
    )
    mid_coef = 0.5 * mid_data + scale_e2 * lax.psum(prolong_part, "row")
    fine_part = listed_terms(
        points0, mid_cols, tiles_e1[0, 0], mid_coef.astype(jnp.bfloat16), support_mid, False
    )
    fine_coef = 0.5 * own_data + scale_e1 * lax.psum_scatter(
        fine_part, "col", scatter_dimension=0, tiled=True
    )
    fine_total = lax.psum(fine_square / col_count, ("row", "col"))
    fine_norm = fine_total / (rows_fine * row_count * fields)
    return (fine_coef, mid_coef, coarse_coef, jnp.stack([fine_norm]))


def solution(mesh):
    return jax.shard_map(
        per_device,
        mesh=mesh,
        in_specs=(
            P("row", None),
            P(None, "row"),
            P(None, "row"),
            P(None, "row"),
            P("row", "col", None, None),
            P("row", "col", None, None),
            P("row", "col", None, None),
            P("row", "col"),
        ),
        out_specs=(P(("row", "col"), None), P("col", None), P("row", None), P()),
        check_vma=False,
    )
```

profile of v0, /device:TPU:0, one launch (start us, length us, event | category | flops | bytes accessed | tf_op | source)
XLA Modules:
  0.0 501.4 jit_solution(3732552858694689181)
XLA Ops:
  7.3 1.7 dynamic-slice_select_fusion
  11.9 8.5 %all-reduce = (bf16[2,256]{1,0:T(2,128)(2,1)S(1)}, bf16[2,8,128]{2,0,1:T(2,128)(2,1)S(1)}) all-reduce(bf16[2,256]{1,0:T(2,128)(2,1)S(1)} %broadcast_select_fusion.1, bf16[2,8,128]{2,0,1:T(2,128)(2,1)S(1)} %fusion.64), channel_id=1, replica_groups=mesh['row'=4,'col'=8] {'row'}, use_global_device_ids=true, to_apply=%region_0.1 | all-reduce | flops 2560 | bytes 10240 | tf_op jit(solution)/shard_map/psum | solution.py:15
  20.4 24.9 %all-reduce.8.cloned.1.call-done = bf16[8,128,128]{2,1,0:T(8,128)(2,1)} async-done(((bf16[8,128,128]{2,1,0:T(8,128)(2,1)}), bf16[8,128,128]{2,1,0:T(8,128)(2,1)}) %all-reduce.8.cloned.1.call-update) | async-done | bytes 262160 | tf_op jit(solution)/shard_map/psum | solution.py:15
  46.3 15.2 %while.40 = (s32[]{:T(128)}, f32[16,128,128]{2,1,0:T(8,128)S(1)}, s32[3,16]{1,0:T(4,128)S(1)}, bf16[2,16,128]{2,0,1:T(2,128)(2,1)S(1)}, s32[3,16]{1,0:T(4,128)S(...) while((s32[]{:T(128)}, f32[16,128,128]{2,1,0:T(8,128)S(1)}, ...), condition=%wide.region_5.6_spmd, body=%wide.region_3.5_spmd.sunk | while | flops 71051360 | bytes 5956313 | solution.py:53
  48.2 1.5 fusion.118
  49.7 1.6 scatter_fusion
  54.8 1.6 scatter_fusion
  59.9 1.6 scatter_fusion
  63.9 77.0 %all-reduce.10.cloned.1.call-done = f32[2048,128]{1,0:T(8,128)} async-done(((f32[2048,128]{1,0:T(8,128)}), f32[2048,128]{1,0:T(8,128)}) %all-reduce.10.cloned.1.call-update) | async-done | bytes 1048592 | tf_op jit(solution)/shard_map/psum | solution.py:84
  140.9 2.2 multiply_reduce_fusion
  143.1 14.7 %while.41 = (s32[]{:T(128)}, f32[2,128,128]{2,1,0:T(8,128)S(1)}, s32[5,4]{1,0:T(8,128)S(1)}, s32[5,4]{1,0:T(8,128)S(1)}, bf16[2,16,128]{2,0,1:T(2,128)(2,1)S(1)}...) while((s32[]{:T(128)}, f32[2,128,128]{2,1,0:T(8,128)S(1)}, ...), condition=%wide.region_9.10_spmd, body=%wide.region_7.9_spmd.sunk | while | flops 17764376 | bytes 1495289 | solution.py:53
  158.6 31.5 %all-reduce.12.cloned.1.call-done = f32[256,128]{1,0:T(8,128)} async-done(((f32[256,128]{1,0:T(8,128)}), f32[256,128]{1,0:T(8,128)}) %all-reduce.12.cloned.1.call-update) | async-done | bytes 131088 | tf_op jit(solution)/shard_map/psum | solution.py:90
  193.5 71.1 %all-reduce.14.cloned.1.call-done = f32[512,128]{1,0:T(8,128)} async-done(((f32[512,128]{1,0:T(8,128)}), f32[512,128]{1,0:T(8,128)}) %all-reduce.14.cloned.1.call-update) | async-done | bytes 262160 | tf_op jit(solution)/shard_map/psum | solution.py:95
  264.6 1.6 fusion.57
  266.2 31.9 %all-reduce.16.cloned.1.call-done = bf16[256,128]{1,0:T(8,128)(2,1)} async-done(((bf16[256,128]{1,0:T(8,128)(2,1)}), bf16[256,128]{1,0:T(8,128)(2,1)}) %all-reduce.16.cloned.1.call-update) | async-done | bytes 65552 | tf_op jit(solution)/shard_map/psum | solution.py:15
  299.2 37.1 %psum.91 = f32[64,128]{1,0:T(8,128)S(1)} all-reduce(f32[64,128]{1,0:T(8,128)S(1)} %fusion.56), channel_id=1, replica_groups=mesh['row'=4,'col'=8] {'col'}, use_global_device_ids=true, to_apply=%region_14.15 | all-reduce | flops 8192 | bytes 65536 | tf_op jit(solution)/shard_map/psum | solution.py:103
  336.5 10.8 %psum.92 = bf16[32,128]{0,1:T(8,128)(2,1)S(1)} all-reduce(f32[32,128]{0,1:T(8,128)S(1)} %convolution_bitcast_fusion), channel_id=1, replica_groups=mesh['row'=4,'col'=8] {'row'}, use_global_device_ids=true, to_apply=%region_15.16 | all-reduce | flops 4096 | bytes 24576 | tf_op jit(solution)/shard_map/psum | solution.py:108
  347.5 33.0 %psum.93 = f32[64,128]{1,0:T(8,128)S(1)} all-reduce(f32[64,128]{1,0:T(8,128)S(1)} %convolution_bitcast_fusion.1), channel_id=1, replica_groups=mesh['row'=4,'col'=8] {'col'}, use_global_device_ids=true, to_apply=%region_16.17 | all-reduce | flops 8192 | bytes 65536 | tf_op jit(solution)/shard_map/psum | solution.py:110
  381.6 28.0 %all-reduce.18.cloned.1.call-done = f32[256,128]{1,0:T(8,128)} async-done(((f32[256,128]{1,0:T(8,128)}), f32[256,128]{1,0:T(8,128)}) %all-reduce.18.cloned.1.call-update) | async-done | bytes 131088 | tf_op jit(solution)/shard_map/psum | solution.py:117
  409.5 1.6 fusion.82
  411.2 14.8 %while.42 = (s32[]{:T(128)}, f32[16,128,128]{2,1,0:T(8,128)S(1)}, s32[5,4]{1,0:T(8,128)S(1)}, bf16[2,16,128]{2,0,1:T(2,128)(2,1)S(1)}, s32[5,4]{1,0:T(8,128)S(1)...) while((s32[]{:T(128)}, f32[16,128,128]{2,1,0:T(8,128)S(1)}, ...), condition=%wide.region_20.21_spmd, body=%wide.region_18.20_spmd.sunk | while | flops 17764376 | bytes 1495289 | solution.py:53
  427.7 39.5 %psum.95 = f32[]{:T(128)} all-reduce(f32[]{:T(128)S(6)} %div.39), channel_id=1, replica_groups=mesh['row'=4,'col'=8] {'row','col'}, use_global_device_ids=true, to_apply=%region_23.24 | all-reduce | flops 1 | bytes 8 | tf_op jit(solution)/shard_map/psum | solution.py:124
  467.8 24.0 %reduce-scatter.2.cloned.1.call-done = f32[256,128]{1,0:T(8,128)} async-done(((f32[2048,128]{1,0:T(8,128)}), f32[256,128]{1,0:T(8,128)}) %reduce-scatter.2.cloned.1.call-update) | async-done | bytes 131088 | tf_op jit(solution)/shard_map/reduce_scatter | solution.py:121
  491.8 1.6 multiply_add_fusion
  (228 shorter events, 51.4 us)
Async XLA Ops:
  7.2 329.1 %copy-start = (bf16[64,32]{0,1:T(8,128)(2,1)S(1)}, bf16[64,32]{0,1:T(8,128)(2,1)}, u32[]{:S(2)}) copy-start(bf16[64,32]{0,1:T(8,128)(2,1)} %param.21) | copy-start | bytes 12292
  7.2 38.2 %all-reduce.8.cloned.1.call-start = ((), (), s32[]{:S(2)}) async-start(), calls=%async_computation.1 | async-start | bytes 524288 | tf_op jit(solution)/shard_map/psum | solution.py:15
  9.0 131.9 %all-reduce.10.cloned.1.call-start = ((), (), s32[]{:S(2)}) async-start(), calls=%async_computation.2 | async-start | bytes 2097152 | tf_op jit(solution)/shard_map/psum | solution.py:84
  9.0 0.7 copy-start.11
  9.7 0.7 copy-start.12
  10.4 0.7 copy-start.10
  11.2 0.7 copy-start.8
  45.4 0.9 copy-start.2
  61.5 1.0 copy-start.1
  61.5 1.1 copy-start.13
  61.6 79.4 %copy-start.6 = (bf16[2048,128]{1,0:T(8,128)(2,1)S(1)}, bf16[2048,128]{1,0:T(8,128)(2,1)}, u32[]{:S(2)}) copy-start(bf16[2048,128]{1,0:T(8,128)(2,1)} %param.14) | copy-start | bytes 1572868
  62.6 127.5 %all-reduce.12.cloned.1.call-start = ((), (), s32[]{:S(2)}) async-start(), calls=%async_computation.3 | async-start | bytes 262144 | tf_op jit(solution)/shard_map/psum | solution.py:90
  157.9 0.7 copy-start.3
  158.5 106.1 %all-reduce.14.cloned.1.call-start = ((), (), s32[]{:S(2)}) async-start(), calls=%async_computation.4 | async-start | bytes 524288 | tf_op jit(solution)/shard_map/psum | solution.py:95
  192.7 0.7 copy-start.5
  192.7 0.8 copy-start.14
  193.4 104.7 %all-reduce.16.cloned.1.call-start = ((), (), s32[]{:S(2)}) async-start(), calls=%async_computation.5 | async-start | bytes 131072 | tf_op jit(solution)/shard_map/psum | solution.py:15
  193.5 104.6 %copy-start.7 = (f32[256,128]{1,0:T(8,128)S(1)}, f32[256,128]{1,0:T(8,128)}, u32[]{:S(2)}) copy-start(f32[256,128]{1,0:T(8,128)} %all-reduce.12.cloned.1.call-done) | copy-start | bytes 393220
  266.2 143.4 %all-reduce.18.cloned.1.call-start = ((), (), s32[]{:S(2)}) async-start(), calls=%async_computation.6 | async-start | bytes 262144 | tf_op jit(solution)/shard_map/psum | solution.py:117
  380.5 1.0 copy-start.9
  381.5 110.3 %reduce-scatter.2.cloned.1.call-start = ((), (), s32[]{:S(2)}) async-start(), calls=%async_computation.7 | async-start | bytes 1179648 | tf_op jit(solution)/shard_map/reduce_scatter | solution.py:121
  426.0 1.0 copy-start.4
Sparse Core Ops, SparseCore 0:
  10.3 34.9 all-reduce.7
  62.7 78.1 all-reduce.9
  158.7 31.3 all-reduce.11
  193.6 70.9 all-reduce.13
  267.3 30.7 all-reduce.15
  381.6 27.8 all-reduce.17
  427.2 64.5 reduce-scatter.1
where the time goes:
time: 502 us; the launch traced here: 501 us
  waiting for transfers between devices  288 us (57%)
  blocking collectives  129 us (26%)
  local copies, waits for them, and re-layouts  31.9 us (6%)
  other arithmetic  23.1 us (5%)
  between operations  16.8 us (3%)
  matrix products  10.9 us (2%)
    psum x1, waiting for transfers between devices, per_device(): product_whole = lax.psum(product_part, 'col')  77 us
    psum x1, waiting for transfers between devices, per_device(): mid_whole = (scale_a1 * lax.psum(mid_part, 'col')).astype(jnp.bfloat16)  71.1 us
    psum x2, waiting for transfers between devices, spread(): return lax.psum(jnp.where(mine, x, jnp.zeros_like(x)), axis)  56.8 us
    psum x1, blocking collectives, per_device(): fine_total = lax.psum(fine_square / col_count, ('row', 'col'))  39.5 us
    psum x1, blocking collectives, per_device(): coarse_sum = lax.psum(coarse_part, 'col')  37.1 us
    psum x1, blocking collectives, per_device(): coarse_coef = lax.psum(coarse_part_two, 'col')  33 us
    psum x1, waiting for transfers between devices, per_device(): restrict_sum = lax.psum(restrict_part, 'row')  31.5 us
    psum x1, waiting for transfers between devices, per_device(): mid_coef = 0.5 * mid_data + scale_e2 * lax.psum(prolong_part, 'row')  28 us
  transfers between devices with their start and end apart: 7, of which 7 were waited for; matrix products, arithmetic and copies ran while one was open for 0% of the time, Pallas kernels for 0%

commit v1 on v0

--- a/solution.py
+++ b/solution.py
@@ -107,7 +107,11 @@
     )
     halfway = lax.psum(halfway_part, "row").astype(jnp.bfloat16)
     coarse_part_two = jnp.dot(factor, halfway, preferred_element_type=jnp.float32)
-    coarse_coef = lax.psum(coarse_part_two, "col")
+    coarse_coef = coarse_part_two
+    for hop in (1, 2, 4):
+        coarse_coef = coarse_coef + lax.ppermute(
+            coarse_coef, "col", [(dev, dev ^ hop) for dev in range(8)]
+        )
     prolong_part = lax.dot_general(
         coarse_kernel,
         coarse_coef.astype(jnp.bfloat16),

time: 502 us -> 481 us (0.958)
  blocking collectives: 129 us -> 96 us
  waiting for transfers between devices: 288 us -> 301 us
    psum x1 -> x0, blocking collectives: 33 us -> none  [per_device(): coarse_coef = lax.psum(coarse_part_two, 'col')]
    ppermute x0 -> x3, waiting for transfers between devices: none -> 12.6 us  [per_device(): lax.ppermute(coarse_coef, 'col', [(dev, dev ^ hop) for dev in range(8)])]
  transfers between devices with their start and end apart: 7 -> 10, of which waited for: 7 -> 10; matrix products, arithmetic and copies ran while one was open for 0% -> 0% of each run, Pallas kernels for 0% -> 0%
where the time goes in v1:
time: 481 us
  waiting for transfers between devices  301 us (63%)
  blocking collectives  96 us (20%)
  local copies, waits for them, and re-layouts  31.8 us (7%)
  other arithmetic  23.1 us (5%)
  between operations  16.8 us (3%)
  matrix products  11 us (2%)
    psum x1, waiting for transfers between devices, per_device(): product_whole = lax.psum(product_part, 'col')  77.1 us
    psum x1, waiting for transfers between devices, per_device(): mid_whole = (scale_a1 * lax.psum(mid_part, 'col')).astype(jnp.bfloat16)  71.1 us
    psum x2, waiting for transfers between devices, spread(): return lax.psum(jnp.where(mine, x, jnp.zeros_like(x)), axis)  56.8 us
    psum x1, blocking collectives, per_device(): fine_total = lax.psum(fine_square / col_count, ('row', 'col'))  39.5 us
    psum x1, blocking collectives, per_device(): coarse_sum = lax.psum(coarse_part, 'col')  37.1 us
    psum x1, waiting for transfers between devices, per_device(): restrict_sum = lax.psum(restrict_part, 'row')  31.5 us
    psum x1, waiting for transfers between devices, per_device(): mid_coef = 0.5 * mid_data + scale_e2 * lax.psum(prolong_part, 'row')  28 us
    reduce_scatter x1, waiting for transfers between devices, per_device(): lax.psum_scatter(fine_part, 'col', scatter_dimension=0, tiled=True)  23.7 us
  transfers between devices with their start and end apart: 10, of which 10 were waited for; matrix products, arithmetic and copies ran while one was open for 0% of the time, Pallas kernels for 0%

profile of v1, /device:TPU:0, one launch (start us, length us, event | category | flops | bytes accessed | tf_op | source)
XLA Modules:
  0.0 480.7 jit_solution(11339235179764697048)
XLA Ops:
  7.3 1.7 dynamic-slice_select_fusion
  11.9 8.5 %all-reduce = (bf16[2,256]{1,0:T(2,128)(2,1)S(1)}, bf16[2,8,128]{2,0,1:T(2,128)(2,1)S(1)}) all-reduce(bf16[2,256]{1,0:T(2,128)(2,1)S(1)} %broadcast_select_fusion.1, bf16[2,8,128]{2,0,1:T(2,128)(2,1)S(1)} %fusion.64), channel_id=1, replica_groups=mesh['row'=4,'col'=8] {'row'}, use_global_device_ids=true, to_apply=%region_0.1 | all-reduce | flops 2560 | bytes 10240 | tf_op jit(solution)/shard_map/psum | solution.py:15
  20.4 24.9 %all-reduce.8.cloned.1.call-done = bf16[8,128,128]{2,1,0:T(8,128)(2,1)} async-done(((bf16[8,128,128]{2,1,0:T(8,128)(2,1)}), bf16[8,128,128]{2,1,0:T(8,128)(2,1)}) %all-reduce.8.cloned.1.call-update) | async-done | bytes 262160 | tf_op jit(solution)/shard_map/psum | solution.py:15
  46.3 15.2 %while.40 = (s32[]{:T(128)}, f32[16,128,128]{2,1,0:T(8,128)S(1)}, s32[3,16]{1,0:T(4,128)S(1)}, bf16[2,16,128]{2,0,1:T(2,128)(2,1)S(1)}, s32[3,16]{1,0:T(4,128)S(...) while((s32[]{:T(128)}, f32[16,128,128]{2,1,0:T(8,128)S(1)}, ...), condition=%wide.region_5.6_spmd, body=%wide.region_3.5_spmd.sunk | while | flops 71051360 | bytes 5956313 | solution.py:53
  49.7 1.6 scatter_fusion
  54.8 1.6 scatter_fusion
  59.9 1.6 scatter_fusion
  63.9 77.1 %all-reduce.10.cloned.1.call-done = f32[2048,128]{1,0:T(8,128)} async-done(((f32[2048,128]{1,0:T(8,128)}), f32[2048,128]{1,0:T(8,128)}) %all-reduce.10.cloned.1.call-update) | async-done | bytes 1048592 | tf_op jit(solution)/shard_map/psum | solution.py:84
  140.9 2.1 multiply_reduce_fusion
  143.1 14.7 %while.41 = (s32[]{:T(128)}, f32[2,128,128]{2,1,0:T(8,128)S(1)}, s32[5,4]{1,0:T(8,128)S(1)}, s32[5,4]{1,0:T(8,128)S(1)}, bf16[2,16,128]{2,0,1:T(2,128)(2,1)S(1)}...) while((s32[]{:T(128)}, f32[2,128,128]{2,1,0:T(8,128)S(1)}, ...), condition=%wide.region_9.10_spmd, body=%wide.region_7.9_spmd.sunk | while | flops 17764376 | bytes 1495289 | solution.py:53
  158.6 31.5 %all-reduce.12.cloned.1.call-done = f32[256,128]{1,0:T(8,128)} async-done(((f32[256,128]{1,0:T(8,128)}), f32[256,128]{1,0:T(8,128)}) %all-reduce.12.cloned.1.call-update) | async-done | bytes 131088 | tf_op jit(solution)/shard_map/psum | solution.py:90
  193.5 71.1 %all-reduce.14.cloned.1.call-done = f32[512,128]{1,0:T(8,128)} async-done(((f32[512,128]{1,0:T(8,128)}), f32[512,128]{1,0:T(8,128)}) %all-reduce.14.cloned.1.call-update) | async-done | bytes 262160 | tf_op jit(solution)/shard_map/psum | solution.py:95
  266.2 31.9 %all-reduce.16.cloned.1.call-done = bf16[256,128]{1,0:T(8,128)(2,1)} async-done(((bf16[256,128]{1,0:T(8,128)(2,1)}), bf16[256,128]{1,0:T(8,128)(2,1)}) %all-reduce.16.cloned.1.call-update) | async-done | bytes 65552 | tf_op jit(solution)/shard_map/psum | solution.py:15
  299.2 37.1 %psum.84 = f32[64,128]{1,0:T(8,128)S(1)} all-reduce(f32[64,128]{1,0:T(8,128)S(1)} %fusion.56), channel_id=1, replica_groups=mesh['row'=4,'col'=8] {'col'}, use_global_device_ids=true, to_apply=%region_14.15 | all-reduce | flops 8192 | bytes 65536 | tf_op jit(solution)/shard_map/psum | solution.py:103
  336.4 10.8 %psum.85 = bf16[32,128]{0,1:T(8,128)(2,1)S(1)} all-reduce(f32[32,128]{0,1:T(8,128)S(1)} %convolution_bitcast_fusion), channel_id=1, replica_groups=mesh['row'=4,'col'=8] {'row'}, use_global_device_ids=true, to_apply=%region_15.16 | all-reduce | flops 4096 | bytes 24576 | tf_op jit(solution)/shard_map/psum | solution.py:108
  347.5 3.9 collective-permute-done
  351.4 3.9 collective-permute-done.1
  355.3 4.8 collective-permute-done.2
  361.2 28.0 %all-reduce.18.cloned.1.call-done = f32[256,128]{1,0:T(8,128)} async-done(((f32[256,128]{1,0:T(8,128)}), f32[256,128]{1,0:T(8,128)}) %all-reduce.18.cloned.1.call-update) | async-done | bytes 131088 | tf_op jit(solution)/shard_map/psum | solution.py:121
  389.2 1.6 fusion.82
  390.9 14.8 %while.42 = (s32[]{:T(128)}, f32[16,128,128]{2,1,0:T(8,128)S(1)}, s32[5,4]{1,0:T(8,128)S(1)}, bf16[2,16,128]{2,0,1:T(2,128)(2,1)S(1)}, s32[5,4]{1,0:T(8,128)S(1)...) while((s32[]{:T(128)}, f32[16,128,128]{2,1,0:T(8,128)S(1)}, ...), condition=%wide.region_19.20_spmd, body=%wide.region_17.19_spmd.sunk | while | flops 17764376 | bytes 1495289 | solution.py:53
  407.3 39.5 %psum.87 = f32[]{:T(128)} all-reduce(f32[]{:T(128)S(6)} %div.39), channel_id=1, replica_groups=mesh['row'=4,'col'=8] {'row','col'}, use_global_device_ids=true, to_apply=%region_22.23 | all-reduce | flops 1 | bytes 8 | tf_op jit(solution)/shard_map/psum | solution.py:128
  447.4 23.7 %reduce-scatter.2.cloned.1.call-done = f32[256,128]{1,0:T(8,128)} async-done(((f32[2048,128]{1,0:T(8,128)}), f32[256,128]{1,0:T(8,128)}) %reduce-scatter.2.cloned.1.call-update) | async-done | bytes 131088 | tf_op jit(solution)/shard_map/reduce_scatter | solution.py:125
  471.1 1.6 multiply_add_fusion
  (236 shorter events, 54.4 us)
Async XLA Ops:
  7.2 329.1 %copy-start = (bf16[64,32]{0,1:T(8,128)(2,1)S(1)}, bf16[64,32]{0,1:T(8,128)(2,1)}, u32[]{:S(2)}) copy-start(bf16[64,32]{0,1:T(8,128)(2,1)} %param.21) | copy-start | bytes 12292
  7.2 38.2 %all-reduce.8.cloned.1.call-start = ((), (), s32[]{:S(2)}) async-start(), calls=%async_computation.1 | async-start | bytes 524288 | tf_op jit(solution)/shard_map/psum | solution.py:15
  9.0 131.9 %all-reduce.10.cloned.1.call-start = ((), (), s32[]{:S(2)}) async-start(), calls=%async_computation.2 | async-start | bytes 2097152 | tf_op jit(solution)/shard_map/psum | solution.py:84
  9.0 0.7 copy-start.11
  9.7 0.7 copy-start.12
  10.4 0.7 copy-start.10
  11.2 0.7 copy-start.8
  45.4 0.9 copy-start.2
  61.5 1.0 copy-start.1
  61.5 1.1 copy-start.13
  61.6 79.4 %copy-start.6 = (bf16[2048,128]{1,0:T(8,128)(2,1)S(1)}, bf16[2048,128]{1,0:T(8,128)(2,1)}, u32[]{:S(2)}) copy-start(bf16[2048,128]{1,0:T(8,128)(2,1)} %param.14) | copy-start | bytes 1572868
  62.6 127.5 %all-reduce.12.cloned.1.call-start = ((), (), s32[]{:S(2)}) async-start(), calls=%async_computation.3 | async-start | bytes 262144 | tf_op jit(solution)/shard_map/psum | solution.py:90
  158.5 106.1 %all-reduce.14.cloned.1.call-start = ((), (), s32[]{:S(2)}) async-start(), calls=%async_computation.4 | async-start | bytes 524288 | tf_op jit(solution)/shard_map/psum | solution.py:95
  192.7 0.7 copy-start.5
  192.7 0.8 copy-start.14
  193.4 104.7 %all-reduce.16.cloned.1.call-start = ((), (), s32[]{:S(2)}) async-start(), calls=%async_computation.5 | async-start | bytes 131072 | tf_op jit(solution)/shard_map/psum | solution.py:15
  193.5 104.6 %copy-start.7 = (f32[256,128]{1,0:T(8,128)S(1)}, f32[256,128]{1,0:T(8,128)}, u32[]{:S(2)}) copy-start(f32[256,128]{1,0:T(8,128)} %all-reduce.12.cloned.1.call-done) | copy-start | bytes 393220
  266.2 123.0 %all-reduce.18.cloned.1.call-start = ((), (), s32[]{:S(2)}) async-start(), calls=%async_computation.6 | async-start | bytes 262144 | tf_op jit(solution)/shard_map/psum | solution.py:121
  347.5 3.9 collective-permute-start
  351.4 3.9 collective-permute-start.1
  355.3 4.8 %collective-permute-start.2 = (f32[64,128]{1,0:T(8,128)S(1)}, f32[64,128]{1,0:T(8,128)S(1)}, u32[]{:S(2)}, u32[]{:S(2)}) collective-permute-start(f32[64,128]{1,0:T(8,128)S(1)} %add.252), channel_id=1, source_target_pairs={{0,4},{1,5},{2,6},{3,7},{4,0},{5,1},{6,2},{7,3},{8,12},{9,13},{10,... | collective-permute-start | bytes 98312 | tf_op jit(solution)/shard_map/ppermute | solution.py:112
  360.2 1.0 copy-start.9
  361.1 109.9 %reduce-scatter.2.cloned.1.call-start = ((), (), s32[]{:S(2)}) async-start(), calls=%async_computation.7 | async-start | bytes 1179648 | tf_op jit(solution)/shard_map/reduce_scatter | solution.py:125
  405.6 1.0 copy-start.4
  (1 other events, 0.7 us)
Sparse Core Ops, SparseCore 0:
  10.3 34.9 all-reduce.7
  62.7 78.1 all-reduce.9
  158.6 31.3 all-reduce.11
  193.5 71.0 all-reduce.13
  267.3 30.7 all-reduce.15
  361.3 27.8 all-reduce.17
  406.8 64.2 reduce-scatter.1
